TPU v7x, 32 devices: a whole 2x2x4 slice. The times are simulated.
32 devices in a mesh: dp: 2 (over y), ep: 16 (over z, x, core).
Axes of the slice: x: 2, y: 2, z: 4, core: 2. Of those that a mesh axis runs over, the one named last changes fastest.
Arguments:
- tokens: bfloat16 [16, 2, 1, 3584], P('ep', 'dp'), may hold values from -6 to 6
- gate_weights: bfloat16 [16, 2, 1, 8], P('ep', 'dp'), may hold values from 0.099609375 to 0.59765625
- expert_ids: int32 [16, 2, 1, 8], P('ep', 'dp'), may hold values from 0 to 15, all different within a row; in each aligned block of 2 rows (0 to 1, 2 to 3, ..., all dimensions but the last counted through in order) at most 2 rows name the same one
- gate_proj: bfloat16 [16, 3584, 2048], P('ep', None, 'dp'), may hold values from -0.09375 to 0.09375
- up_proj: bfloat16 [16, 3584, 2048], P('ep', None, 'dp'), may hold values from -0.09375 to 0.09375
- down_proj: bfloat16 [16, 2048, 3584], P('ep', 'dp'), may hold values from -0.125 to 0.125
Outputs:
- mixed: bfloat16 [16, 2, 1, 3584], P('ep', 'dp')
Inputs may be any that keep to these rules, and one draw needn't show every extreme that they name: `expert_ids`: each token names 8 different experts. Among the 2 tokens of one index of the first dimension, no expert is named more than 2 times, a bound that some block reaches.
All inputs are finite; a program needn't handle non-finite values.
Results may differ from a plain program's by a relative error of at most 0.02.
Values may be sent and summed in bfloat16 or wider, within the bound.
A program may use at most 64 MiB of HBM per device.

v0:
```python
import jax
import jax.numpy as jnp
from jax import lax
from jax.sharding import PartitionSpec as P


def placing(flat_ids, expert_count, capacity):
    labels = jnp.arange(expert_count, dtype=jnp.int32)
    onehot = (flat_ids[:, None] == labels[None, :]).astype(jnp.int32)
    earlier = jnp.cumsum(onehot, axis=0) - onehot
    slot_index = jnp.sum(earlier * onehot, axis=1)
    destination = flat_ids * capacity + slot_index
    targets = jnp.arange(expert_count * capacity, dtype=jnp.int32)
    return (destination[:, None] == targets[None, :]).astype(jnp.float32)


def body(tokens, gate_weights, expert_ids, gate_proj, up_proj, down_proj):
    group_count = lax.axis_size("dp")
    expert_count = lax.axis_size("ep")
    token_count = tokens.shape[2]
    feature_count = tokens.shape[3]
    top_count = expert_ids.shape[3]
    capacity = min(
        group_count * token_count, token_count * (group_count * top_count // expert_count + 1)
    )
    token_total = group_count * token_count
    slot_total = expert_count * capacity
    column_count = feature_count // group_count
    all_ids = lax.all_gather(expert_ids, "dp", axis=1, tiled=True)
    placed = placing(all_ids.reshape(-1), expert_count, capacity)
    selection = jnp.sum(placed.reshape(token_total, top_count, slot_total), axis=1)
    selection_t = selection.T.astype(jnp.bfloat16)
    token_rows, all_weights = (
        lax.all_gather(tokens, "dp", axis=1, tiled=True),
        lax.all_gather(gate_weights, "dp", axis=1, tiled=True),
    )
    buffer = jnp.dot(
        selection_t,
        token_rows.reshape(token_total, feature_count),
        preferred_element_type=jnp.float32,
    ).astype(jnp.bfloat16)
    received = lax.all_to_all(
        buffer.reshape(expert_count, capacity, feature_count),
        "ep",
        split_axis=0,
        concat_axis=0,
        tiled=True,
    )
    slot_rows = received.reshape(slot_total, feature_count)
    gate_act = jnp.dot(slot_rows, gate_proj[0], preferred_element_type=jnp.float32)
    up_act = jnp.dot(slot_rows, up_proj[0], preferred_element_type=jnp.float32)
    hidden = (jax.nn.silu(gate_act) * up_act).astype(jnp.bfloat16)
    down_mat = down_proj[0]
    summed_t = lax.psum_scatter(
        lax.dot_general(
            down_mat, hidden, (((0,), (1,)), ((), ())), preferred_element_type=jnp.float32
        ).astype(jnp.bfloat16),
        "dp",
        scatter_dimension=0,
        tiled=True,
    ).astype(jnp.float32)
    summed = summed_t.T.astype(jnp.bfloat16).reshape(expert_count, capacity, column_count)
    returned = lax.all_to_all(summed, "ep", split_axis=0, concat_axis=0, tiled=True)
    weight_flat = all_weights.reshape(-1).astype(jnp.float32)
    weighted = jnp.sum(
        (placed * weight_flat[:, None]).reshape(token_total, top_count, slot_total), axis=1
    )
    mixed = jnp.dot(
        weighted,
        returned.reshape(slot_total, column_count).astype(jnp.float32),
        precision=lax.Precision.HIGHEST,
    ).astype(jnp.bfloat16)
    own = lax.all_to_all(
        mixed.reshape(group_count, token_count, column_count),
        "dp",
        split_axis=0,
        concat_axis=2,
        tiled=True,
    )
    return own.reshape(1, 1, token_count, feature_count)


def solution(mesh):
    placed = (
        P("ep", "dp", None, None),
        P("ep", "dp", None, None),
        P("ep", "dp", None, None),
        P("ep", None, "dp"),
        P("ep", None, "dp"),
        P("ep", "dp", None),
    )
    return jax.shard_map(
        body, mesh=mesh, in_specs=placed, out_specs=P("ep", "dp", None, None), check_vma=False
    )
```

profile of v0, /device:TPU:0, one launch (start us, length us, event | category | flops | bytes accessed | tf_op | source)
XLA Modules:
  0.0 90.4 jit_solution(14572636809706801968)
XLA Ops:
  6.5 0.0 reduce-scatter.2.cloned.1.call-start
  6.5 5.4 %all_gather.9 = s32[1,2,1,8]{3,2,0,1:T(1,128)S(1)} all-gather(s32[1,1,1,8]{3,2,0,1:T(1,128)} %bitcast.43), channel_id=1, replica_groups=mesh['dp'=2,'ep'=16] {'dp'}, dimensions={1}, use_global_device_ids=true | all-gather | bytes 96 | tf_op jit(solution)/shard_map/all_gather | solution.py:29
  11.9 0.5 broadcast.39
  12.4 0.7 fusion.32
  13.1 0.1 eq.30
  13.2 0.1 fusion.29
  13.3 0.2 select_reduce_fusion.1
  13.5 0.1 reduce_sum.30
  13.6 4.4 %all_gather.10 = bf16[1,2,1,8]{3,2,0,1:T(2,128)(2,1)S(1)} all-gather(bf16[1,1,1,8]{3,2,0,1:T(2,128)(2,1)} %bitcast.44), channel_id=1, replica_groups=mesh['dp'=2,'ep'=16] {'dp'}, dimensions={1}, use_global_device_ids=true | all-gather | bytes 48 | tf_op jit(solution)/shard_map/all_gather | solution.py:35
  17.9 4.6 %all_gather.11 = bf16[1,2,1,3584]{3,2,0,1:T(2,128)(2,1)S(1)} all-gather(bf16[1,1,1,3584]{3,2,0,1:T(2,128)(2,1)} %bitcast.40), channel_id=1, replica_groups=mesh['dp'=2,'ep'=16] {'dp'}, dimensions={1}, use_global_device_ids=true | all-gather | bytes 21504 | tf_op jit(solution)/shard_map/all_gather | solution.py:34
  22.6 0.1 convert_reduce_fusion
  22.6 0.3 convolution_convert_fusion
  22.9 0.1 reshape.70
  23.0 15.6 %all_to_all.19 = bf16[16,2,3584]{2,1,0:T(2,128)(2,1)S(1)} all-to-all(bf16[16,2,3584]{2,1,0:T(2,128)(2,1)S(1)} %reshape.70), channel_id=1, replica_groups=mesh['dp'=2,'ep'=16] {'ep'}, dimensions={0} | all-to-all | bytes 458752 | tf_op jit(solution)/shard_map/all_to_all | solution.py:42
  38.7 0.1 reshape.71
  38.7 4.4 %fusion.4 = f32[32,1024]{1,0:T(8,128)S(1)} fusion(bf16[32,3584]{1,0:T(8,128)(2,1)S(1)} %reshape.71, bf16[1,3584,1024]{2,1,0:T(8,128)(2,1)} %param.9), kind=kOutput, calls=%fused_computation.4 | convolution fusion | flops 234881024 | bytes 7700480 | tf_op jit(solution)/shard_map/dot_general | solution.py:50
  43.2 8.5 %fusion.9 = bf16[3584,32]{0,1:T(8,128)(2,1)} fusion(bf16[1,1024,3584]{2,1,0:T(8,128)(2,1)} %param.11, bf16[32,3584]{1,0:T(8,128)(2,1)S(1)} %reshape.71, bf16[1,3584,1024]{2,1,0:T(8,128)(2,1)} %param.10, f32[32,1024]{1,0:T(8,128)S(1)} %fusion.4), kind=kOutput, calls=%fused_computation.8 | convolution fusion | flops 470073344 | bytes 15269888 | tf_op jit(solution)/shard_map/dot_general | solution.py:55
  51.7 0.0 reduce-scatter.2.cloned.1.call-update
  51.7 9.6 %reduce-scatter.2.cloned.1.call-done = bf16[1792,32]{0,1:T(8,128)(2,1)} async-done(((bf16[3584,32]{0,1:T(8,128)(2,1)}), bf16[1792,32]{0,1:T(8,128)(2,1)}) %reduce-scatter.2.cloned.1.call-update) | async-done | bytes 114704 | tf_op jit(solution)/shard_map/reduce_scatter | solution.py:54
  61.3 0.9 %reshape.72 = bf16[16,2,1792]{2,1,0:T(2,128)(2,1)S(1)} reshape(bf16[32,1792]{1,0:T(8,128)(2,1)} %bitcast.39) | data formatting | bytes 229376 | tf_op jit(solution)/shard_map/reshape | solution.py:62
  62.3 13.0 %all_to_all.20 = bf16[16,2,1792]{2,1,0:T(2,128)(2,1)S(1)} all-to-all(bf16[16,2,1792]{2,1,0:T(2,128)(2,1)S(1)} %reshape.72), channel_id=1, replica_groups=mesh['dp'=2,'ep'=16] {'ep'}, dimensions={0} | all-to-all | bytes 229376 | tf_op jit(solution)/shard_map/all_to_all | solution.py:63
  75.4 0.2 fusion.12
  75.6 0.5 broadcast.40
  76.1 0.7 reduce.5
  76.8 6.1 %all_to_all.21 = bf16[2,2,896]{2,1,0:T(2,128)(2,1)S(1)} all-to-all(bf16[2,2,896]{2,1,0:T(2,128)(2,1)S(1)} %reshape.86), channel_id=1, replica_groups=mesh['dp'=2,'ep'=16] {'dp'}, dimensions={0} | all-to-all | bytes 14336 | tf_op jit(solution)/shard_map/all_to_all | solution.py:73
  82.9 0.6 reshape.87
  (5 shorter events, 0.1 us)
Async XLA Ops:
  6.5 54.8 %reduce-scatter.2.cloned.1.call-start = ((), (), s32[]{:S(2)}) async-start(), calls=%async_computation.4 | async-start | bytes 344064 | tf_op jit(solution)/shard_map/reduce_scatter | solution.py:54
Sparse Core Ops, SparseCore 0:
  51.8 9.4 reduce-scatter.1
where the time goes:
time: 90.7 us; the launch traced here: 90.4 us
  blocking collectives  49.2 us (54%)
  matrix products  13.4 us (15%)
  between operations  13.4 us (15%)
  waiting for transfers between devices  9.65 us (11%)
  local copies, waits for them, and re-layouts  3 us (3%)
  other arithmetic  1.72 us (2%)
    all_to_all x1, blocking collectives, body(): lax.all_to_all(buffer.reshape(expert_count, capacity, feature_count), 'ep...  15.6 us
    all_to_all x1, blocking collectives, body(): lax.all_to_all(summed, 'ep', split_axis=0, concat_axis=0, tiled=True)  13 us
    reduce_scatter x1, waiting for transfers between devices, body(): lax.psum_scatter(lax.dot_general(down_mat, hidden, (((0,), (1,)), ((), ()...  9.63 us
    dot_general x1, matrix products, body(): lax.dot_general(down_mat, hidden, (((0,), (1,)), ((), ())), preferred_ele...  8.5 us
    all_to_all x1, blocking collectives, body(): lax.all_to_all(mixed.reshape(group_count, token_count, column_count), 'dp...  6.14 us
    all_gather x1, blocking collectives, body(): all_ids = lax.all_gather(expert_ids, 'dp', axis=1, tiled=True)  5.38 us
    all_gather x1, blocking collectives, body(): lax.all_gather(tokens, 'dp', axis=1, tiled=True)  4.61 us
    dot_general x1, matrix products, body(): jnp.dot(slot_rows, gate_proj[0], preferred_element_type=jnp.float32)  4.45 us
  transfers between devices with their start and end apart: 1, of which 1 were waited for; matrix products, arithmetic and copies ran while one was open for 0% of the time, Pallas kernels for 0%

commit v1 on v0

--- a/solution.py
+++ b/solution.py
@@ -1,6 +1,10 @@
+import functools
+
 import jax
 import jax.numpy as jnp
 from jax import lax
+from jax.experimental import pallas as pl
+from jax.experimental.pallas import tpu as pltpu
 from jax.sharding import PartitionSpec as P
 
 
@@ -80,6 +84,241 @@
     return own.reshape(1, 1, token_count, feature_count)
 
 
+LANES = 128
+MESH = pl.DeviceIdType.MESH
+
+
+def kernel(
+    groups,
+    experts,
+    pieces,
+    tok_ref,
+    weight_ref,
+    ids_ref,
+    gate_hbm,
+    up_hbm,
+    down_hbm,
+    out_ref,
+    gate_w,
+    up_w,
+    down_w,
+    own32,
+    own16,
+    rows16,
+    rows32,
+    rows_mat,
+    sent16,
+    got16,
+    gate_sem,
+    up_sem,
+    down_sem,
+    tok_send,
+    tok_recv,
+    res_send,
+    res_recv,
+):
+    total = groups * experts
+    features, hidden_count = gate_hbm.shape
+    blocks = features // LANES
+    pitch = own32.shape[0]
+    step = features // pieces
+
+    gate_copies, up_copies, down_copies = [], [], []
+    for p in range(pieces):
+        part = pl.ds(p * step, step)
+        gate_copies.append(pltpu.make_async_copy(gate_hbm.at[part], gate_w.at[part], gate_sem.at[p]))
+        up_copies.append(pltpu.make_async_copy(up_hbm.at[part], up_w.at[part], up_sem.at[p]))
+        down_copies.append(
+            pltpu.make_async_copy(down_hbm.at[:, part], down_w.at[:, part], down_sem.at[p])
+        )
+    for p in range(pieces):
+        gate_copies[p].start()
+        up_copies[p].start()
+    for p in range(pieces):
+        down_copies[p].start()
+
+    me = lax.axis_index("ep") * groups + lax.axis_index("dp")
+
+    def place(flat):
+        return (flat % groups, flat // groups)
+
+    barrier = pltpu.get_barrier_semaphore()
+
+    def greet(d, carry):
+        pl.semaphore_signal(
+            barrier, inc=1, device_id=place((me + d) % total), device_id_type=MESH
+        )
+        return carry
+
+    lax.fori_loop(1, total, greet, 0)
+
+    own32[...] = jnp.zeros_like(own32)
+    for j in range(blocks):
+        own32[j : j + 1, :] = tok_ref[:, j * LANES : (j + 1) * LANES].astype(jnp.float32)
+    own16[...] = own32[...].astype(jnp.bfloat16)
+
+    pl.semaphore_wait(barrier, total - 1)
+
+    def token_copy(target, slot):
+        return pltpu.make_async_remote_copy(
+            src_ref=own16,
+            dst_ref=rows16.at[slot],
+            send_sem=tok_send.at[target],
+            recv_sem=tok_recv.at[slot],
+            device_id=place(target),
+            device_id_type=MESH,
+        )
+
+    def send_token(d, carry):
+        token_copy((me + d) % total, me).start()
+        return carry
+
+    lax.fori_loop(1, total, send_token, 0)
+    rows16[me] = own16[...]
+
+    def wait_token(d, carry):
+        other = (me + d) % total
+        token_copy(other, other).wait_recv()
+        return carry
+
+    lax.fori_loop(1, total, wait_token, 0)
+
+    for t in range(total):
+        rows32[t * pitch : (t + 1) * pitch, :] = rows16[t].astype(jnp.float32)
+    for j in range(blocks):
+        rows_mat[:, j * LANES : (j + 1) * LANES] = rows32[
+            pl.ds(j, total, stride=pitch), :
+        ].astype(jnp.bfloat16)
+
+    gate_act = jnp.zeros((total, hidden_count), jnp.float32)
+    up_act = jnp.zeros((total, hidden_count), jnp.float32)
+    for p in range(pieces):
+        part = slice(p * step, (p + 1) * step)
+        left = rows_mat[:, part]
+        gate_copies[p].wait()
+        gate_act += jnp.dot(left, gate_w[part, :], preferred_element_type=jnp.float32)
+        up_copies[p].wait()
+        up_act += jnp.dot(left, up_w[part, :], preferred_element_type=jnp.float32)
+    hidden = (gate_act / (1.0 + jnp.exp(-gate_act)) * up_act).astype(jnp.bfloat16)
+
+    for p in range(pieces):
+        down_copies[p].wait()
+        result = jnp.dot(
+            hidden, down_w[:, p * step : (p + 1) * step], preferred_element_type=jnp.float32
+        )
+        for j in range(step // LANES):
+            rows32[pl.ds(p * (step // LANES) + j, total, stride=pitch), :] = result[
+                :, j * LANES : (j + 1) * LANES
+            ]
+    for t in range(total):
+        sent16[t] = rows32[t * pitch : (t + 1) * pitch, :].astype(jnp.bfloat16)
+
+    def result_copy(target, slot):
+        return pltpu.make_async_remote_copy(
+            src_ref=sent16.at[target],
+            dst_ref=got16.at[slot],
+            send_sem=res_send.at[target],
+            recv_sem=res_recv.at[slot],
+            device_id=place(target),
+            device_id_type=MESH,
+        )
+
+    def send_result(d, carry):
+        result_copy((me + d) % total, me).start()
+        return carry
+
+    lax.fori_loop(1, total, send_result, 0)
+    got16[me] = sent16[me]
+
+    labels = lax.broadcasted_iota(jnp.int32, (experts, ids_ref.shape[1]), 0)
+    chosen = jnp.where(ids_ref[...] == labels, weight_ref[...].astype(jnp.float32), 0.0)
+    mix = jnp.broadcast_to(jnp.sum(chosen, axis=1, keepdims=True), (experts, LANES))
+
+    def wait_result(d, carry):
+        other = (me + d) % total
+        result_copy(other, other).wait_recv()
+        return carry
+
+    lax.fori_loop(1, total, wait_result, 0)
+
+    mixed = jnp.zeros((pitch, LANES), jnp.float32)
+    for e in range(experts):
+        both = got16[e * groups].astype(jnp.float32)
+        for g in range(1, groups):
+            both += got16[e * groups + g].astype(jnp.float32)
+        mixed += mix[e : e + 1, :] * both
+    for j in range(blocks):
+        out_ref[:, j * LANES : (j + 1) * LANES] = mixed[j : j + 1, :].astype(jnp.bfloat16)
+
+    def wait_sends(d, carry):
+        other = (me + d) % total
+        token_copy(other, me).wait_send()
+        result_copy(other, me).wait_send()
+        return carry
+
+    lax.fori_loop(1, total, wait_sends, 0)
+
+
+def small_body(tokens, gate_weights, expert_ids, gate_proj, up_proj, down_proj):
+    groups = lax.axis_size("dp")
+    experts = lax.axis_size("ep")
+    total = groups * experts
+    features = tokens.shape[3]
+    top_count = expert_ids.shape[3]
+    hidden_count = gate_proj.shape[2]
+    blocks = features // LANES
+    pitch = -(-blocks // 16) * 16
+    pieces = max(p for p in (7, 4, 2, 1) if blocks % p == 0)
+    vmem = pl.BlockSpec(memory_space=pltpu.VMEM)
+    hbm = pl.BlockSpec(memory_space=pl.ANY)
+    dma = pltpu.SemaphoreType.DMA
+    out = pl.pallas_call(
+        functools.partial(kernel, groups, experts, pieces),
+        out_shape=jax.ShapeDtypeStruct((1, features), jnp.bfloat16),
+        in_specs=[vmem, vmem, vmem, hbm, hbm, hbm],
+        out_specs=vmem,
+        scratch_shapes=[
+            pltpu.VMEM((features, hidden_count), jnp.bfloat16),
+            pltpu.VMEM((features, hidden_count), jnp.bfloat16),
+            pltpu.VMEM((hidden_count, features), jnp.bfloat16),
+            pltpu.VMEM((pitch, LANES), jnp.float32),
+            pltpu.VMEM((pitch, LANES), jnp.bfloat16),
+            pltpu.VMEM((total, pitch, LANES), jnp.bfloat16),
+            pltpu.VMEM((total * pitch, LANES), jnp.float32),
+            pltpu.VMEM((total, features), jnp.bfloat16),
+            pltpu.VMEM((total, pitch, LANES), jnp.bfloat16),
+            pltpu.VMEM((total, pitch, LANES), jnp.bfloat16),
+            dma((pieces,)),
+            dma((pieces,)),
+            dma((pieces,)),
+            dma((total,)),
+            dma((total,)),
+            dma((total,)),
+            dma((total,)),
+        ],
+        compiler_params=pltpu.CompilerParams(collective_id=0, has_side_effects=True),
+    )(
+        tokens.reshape(1, features),
+        gate_weights.reshape(1, top_count),
+        expert_ids.reshape(1, top_count),
+        gate_proj[0],
+        up_proj[0],
+        down_proj[0],
+    )
+    return out.reshape(1, 1, 1, features)
+
+
+def layer(tokens, gate_weights, expert_ids, gate_proj, up_proj, down_proj):
+    groups = lax.axis_size("dp")
+    total = groups * lax.axis_size("ep")
+    held = 3 * gate_proj.size * gate_proj.dtype.itemsize
+    one_each = tokens.shape[2] == 1 and tokens.shape[3] % LANES == 0
+    fits = total <= 64 and total % 16 == 0 and held <= 36 << 20
+    few = groups <= groups * expert_ids.shape[3] // lax.axis_size("ep") + 1
+    form = small_body if one_each and fits and few else body
+    return form(tokens, gate_weights, expert_ids, gate_proj, up_proj, down_proj)
+
+
 def solution(mesh):
     placed = (
         P("ep", "dp", None, None),
@@ -90,5 +329,5 @@
         P("ep", "dp", None),
     )
     return jax.shard_map(
-        body, mesh=mesh, in_specs=placed, out_specs=P("ep", "dp", None, None), check_vma=False
-    )
+        layer, mesh=mesh, in_specs=placed, out_specs=P("ep", "dp", None, None), check_vma=False
+    )

time: 90.7 us -> 30.8 us (0.34)
  blocking collectives: 49.2 us -> 0 us
  Pallas kernels: 0 us -> 29 us
  matrix products: 13.4 us -> 0 us
  between operations: 13.4 us -> 0.01 us
  waiting for transfers between devices: 9.65 us -> 0 us
  other arithmetic: 1.72 us -> 0 us
  local copies, waits for them, and re-layouts: 3 us -> 1.33 us
    all_to_all x3 -> x0, blocking collectives: 34.8 us -> none  [the longest x1 15.6 us: body(): lax.all_to_all(buffer.reshape(expert_count, capacity, feature_count), 'ep...]
    pallas_call x0 -> x1, Pallas kernels: none -> 29 us  [small_body(): pl.pallas_call(functools.partial(kernel, groups, experts, pieces), out_sh...]
    all_gather x3 -> x0, blocking collectives: 14.4 us -> none  [the longest x1 5.38 us: body(): all_ids = lax.all_gather(expert_ids, 'dp', axis=1, tiled=True)]
    dot_general x4 -> x0, matrix products: 13.4 us -> none  [the longest x1 8.5 us: body(): lax.dot_general(down_mat, hidden, (((0,), (1,)), ((), ())), preferred_ele...]
    reduce_scatter x1 -> x0, waiting for transfers between devices: 9.63 us -> none  [body(): lax.psum_scatter(lax.dot_general(down_mat, hidden, (((0,), (1,)), ((), ()...]
    reshape x5 -> x0, local copies, waits for them, and re-layouts: 1.68 us -> none  [the longest x1 0.94 us: body(): summed_t.T.astype(jnp.bfloat16)]
  transfers between devices with their start and end apart: 1 -> 0, of which waited for: 1 -> 0; matrix products, arithmetic and copies ran while one was open for 0% -> 0% of each run, Pallas kernels for 0% -> 0%
where the time goes in v1:
time: 30.8 us; the launch traced here: 30.4 us
  Pallas kernels  29 us (94%)
  local copies, waits for them, and re-layouts  1.33 us (4%)
    pallas_call x1, Pallas kernels, small_body(): pl.pallas_call(functools.partial(kernel, groups, experts, pieces), out_sh...  29 us
    unnamed x1, local copies, waits for them, and re-layouts  1.33 us

profile of v1, /device:TPU:0, one launch (start us, length us, event | category | flops | bytes accessed | tf_op | source)
XLA Modules:
  0.0 30.4 jit_solution(12528376985557063946)
XLA Ops:
  0.0 29.0 %shard_map.64 = bf16[1,3584]{1,0:T(2,128)(2,1)} custom-call(bf16[1,3584]{1,0:T(2,128)(2,1)} %bitcast.11, bf16[1,8]{1,0:T(2,128)(2,1)} %bitcast.12, s32[1,8]{1,0:T(1,128)} %bitcast.13, bf16[3584,1024]{1,0:T(8,128)(2,1)} %bitcast.7, bf16[3584,1024]{1,0:T(8,128)(2,1)} %bitcast.8, bf16[1024,3584]{1,0:T(8,128)(2,1)} %bitcast.9), custom_call_target="tpu_custom_call" | custom-call | tf_op jit(solution)/shard_map/pallas_call | solution.py:275
  29.0 1.3 %copy.8 = bf16[1,1,1,3584]{3,2,1,0:T(2,128)(2,1)} copy(bf16[1,1,1,3584]{3,2,1,0:T(2,128)(2,1)} %bitcast.10) | data formatting | bytes 14336

commit v2 on v1

--- a/solution.py
+++ b/solution.py
@@ -85,6 +85,7 @@
 
 
 LANES = 128
+BAND = 16
 MESH = pl.DeviceIdType.MESH
 
 
@@ -108,12 +109,18 @@
     rows32,
     rows_mat,
     sent16,
+    pair16,
+    halved16,
     got16,
     gate_sem,
     up_sem,
     down_sem,
-    tok_send,
+    line_send,
+    plane_send,
+    share_send,
     tok_recv,
+    pair_send,
+    pair_recv,
     res_send,
     res_recv,
 ):
@@ -122,6 +129,10 @@
     blocks = features // LANES
     pitch = own32.shape[0]
     step = features // pieces
+    cores, across = 2, 2
+    lines = experts // (cores * across)
+    chips = total // cores
+    bands = pitch // BAND
 
     gate_copies, up_copies, down_copies = [], [], []
     for p in range(pieces):
@@ -131,57 +142,107 @@
         down_copies.append(
             pltpu.make_async_copy(down_hbm.at[:, part], down_w.at[:, part], down_sem.at[p])
         )
+
+    my_group = lax.axis_index("dp")
+    my_expert = lax.axis_index("ep")
+    core = my_expert % cores
+    my_across = (my_expert // cores) % across
+    line = my_expert // (cores * across)
+
+    def flat(z, x, c, g):
+        return ((z * across + x) * cores + c) * groups + g
+
+    def where(slot):
+        return (slot % groups, slot // groups)
+
+    def chip_of(slot):
+        return slot // (groups * cores) * groups + slot % groups
+
+    me = flat(line, my_across, core, my_group)
+    partner = flat(line, my_across, 1 - core, my_group)
+    on_line = [flat((line + k) % lines, my_across, core, my_group) for k in range(lines)]
+    near = [
+        ((my_across + i) % across, (my_group + j) % groups)
+        for i in range(across)
+        for j in range(groups)
+        if i or j
+    ]
+    in_plane = [flat(line, x, core, g) for x, g in near]
+
+    barrier = pltpu.get_barrier_semaphore()
+    friends = on_line[1:] + in_plane + [partner]
+    for slot in friends:
+        pl.semaphore_signal(barrier, inc=1, device_id=where(slot), device_id_type=MESH)
+
     for p in range(pieces):
         gate_copies[p].start()
         up_copies[p].start()
     for p in range(pieces):
         down_copies[p].start()
 
-    me = lax.axis_index("ep") * groups + lax.axis_index("dp")
-
-    def place(flat):
-        return (flat % groups, flat // groups)
-
-    barrier = pltpu.get_barrier_semaphore()
-
-    def greet(d, carry):
-        pl.semaphore_signal(
-            barrier, inc=1, device_id=place((me + d) % total), device_id_type=MESH
-        )
-        return carry
-
-    lax.fori_loop(1, total, greet, 0)
-
     own32[...] = jnp.zeros_like(own32)
     for j in range(blocks):
         own32[j : j + 1, :] = tok_ref[:, j * LANES : (j + 1) * LANES].astype(jnp.float32)
+    lane = lax.broadcasted_iota(jnp.int32, (1, LANES), 1)
+    mix = jnp.zeros((1, LANES), jnp.float32)
+    for k in range(ids_ref.shape[1]):
+        mix += jnp.where(
+            lane == ids_ref[:, k : k + 1], weight_ref[:, k : k + 1].astype(jnp.float32), 0.0
+        )
+    own32[blocks : blocks + 1, :] = mix
     own16[...] = own32[...].astype(jnp.bfloat16)
 
-    pl.semaphore_wait(barrier, total - 1)
-
-    def token_copy(target, slot):
+    pl.semaphore_wait(barrier, len(friends))
+
+    def token_copy(source, slot, target, send_sem):
         return pltpu.make_async_remote_copy(
-            src_ref=own16,
+            src_ref=source,
             dst_ref=rows16.at[slot],
-            send_sem=tok_send.at[target],
+            send_sem=send_sem,
             recv_sem=tok_recv.at[slot],
-            device_id=place(target),
+            device_id=where(target),
             device_id_type=MESH,
         )
 
-    def send_token(d, carry):
-        token_copy((me + d) % total, me).start()
-        return carry
-
-    lax.fori_loop(1, total, send_token, 0)
+    sends = []
+
+    def send_token(source, slot, target, send_sem):
+        copy = token_copy(source, slot, target, send_sem)
+        copy.start()
+        sends.append(copy)
+
+    def wait_token(slot):
+        token_copy(own16, slot, slot, line_send.at[0]).wait_recv()
+
+    for k in range(1, lines):
+        send_token(own16, me, on_line[k], line_send.at[k])
+    for q, target in enumerate(in_plane):
+        send_token(own16, me, target, plane_send.at[q])
+    send_token(own16, me, partner, share_send.at[me])
     rows16[me] = own16[...]
 
-    def wait_token(d, carry):
-        other = (me + d) % total
-        token_copy(other, other).wait_recv()
-        return carry
-
-    lax.fori_loop(1, total, wait_token, 0)
+    def reach(k):
+        return [flat((line + k) % lines, x, core, g) for x, g in near]
+
+    order = sorted(range(1, lines), key=lambda k: min(k, lines - k))
+    for slot in reach(0):
+        wait_token(slot)
+        send_token(rows16.at[slot], slot, partner, share_send.at[slot])
+    for k in order:
+        wait_token(on_line[k])
+        for q, target in enumerate(in_plane):
+            send_token(
+                rows16.at[on_line[k]], on_line[k], target, plane_send.at[k * len(near) + q]
+            )
+        send_token(rows16.at[on_line[k]], on_line[k], partner, share_send.at[on_line[k]])
+    for k in order:
+        for slot in reach(k):
+            wait_token(slot)
+            send_token(rows16.at[slot], slot, partner, share_send.at[slot])
+    for k in range(lines):
+        for x in range(across):
+            for g in range(groups):
+                wait_token(flat((line + k) % lines, x, 1 - core, g))
 
     for t in range(total):
         rows32[t * pitch : (t + 1) * pitch, :] = rows16[t].astype(jnp.float32)
@@ -189,6 +250,9 @@
         rows_mat[:, j * LANES : (j + 1) * LANES] = rows32[
             pl.ds(j, total, stride=pitch), :
         ].astype(jnp.bfloat16)
+    mixes = rows32[pl.ds(blocks, total, stride=pitch), :]
+    labels = lax.broadcasted_iota(jnp.int32, (total, LANES), 1)
+    scale = jnp.sum(jnp.where(labels == my_expert, mixes, 0.0), axis=1, keepdims=True)
 
     gate_act = jnp.zeros((total, hidden_count), jnp.float32)
     up_act = jnp.zeros((total, hidden_count), jnp.float32)
@@ -201,62 +265,99 @@
         up_act += jnp.dot(left, up_w[part, :], preferred_element_type=jnp.float32)
     hidden = (gate_act / (1.0 + jnp.exp(-gate_act)) * up_act).astype(jnp.bfloat16)
 
+    def pair_copy(b):
+        rows = pl.ds(b * BAND, BAND)
+        return pltpu.make_async_remote_copy(
+            src_ref=sent16.at[:, 1 - core, :, rows],
+            dst_ref=pair16.at[:, :, rows],
+            send_sem=pair_send.at[b],
+            recv_sem=pair_recv.at[b],
+            device_id=where(partner),
+            device_id_type=MESH,
+        )
+
+    my_chip = chip_of(me)
+
+    def result_copy(target, b, place):
+        rows = pl.ds(b * BAND, BAND)
+        return pltpu.make_async_remote_copy(
+            src_ref=halved16.at[chip_of(target), rows],
+            dst_ref=got16.at[place, rows],
+            send_sem=res_send.at[chip_of(target), b],
+            recv_sem=res_recv.at[place, b],
+            device_id=where(target),
+            device_id_type=MESH,
+        )
+
+    def other_chip(d):
+        h = (my_chip + d) % chips
+        return (h // groups * cores + core) * groups + h % groups
+
+    def pass_on(b):
+        rows = slice(b * BAND, (b + 1) * BAND)
+        pair_copy(b).wait_recv()
+        for h in range(chips):
+            halved16[h, rows] = (
+                sent16[h // groups, core, h % groups, rows].astype(jnp.float32)
+                + pair16[h // groups, h % groups, rows].astype(jnp.float32)
+            ).astype(jnp.bfloat16)
+
+        def send_result(d, carry):
+            result_copy(other_chip(d), b, my_chip).start()
+            return carry
+
+        lax.fori_loop(1, chips, send_result, 0)
+        got16[my_chip, rows] = halved16[my_chip, rows]
+
+    flushed = 0
     for p in range(pieces):
         down_copies[p].wait()
-        result = jnp.dot(
+        result = scale * jnp.dot(
             hidden, down_w[:, p * step : (p + 1) * step], preferred_element_type=jnp.float32
         )
         for j in range(step // LANES):
             rows32[pl.ds(p * (step // LANES) + j, total, stride=pitch), :] = result[
                 :, j * LANES : (j + 1) * LANES
             ]
-    for t in range(total):
-        sent16[t] = rows32[t * pitch : (t + 1) * pitch, :].astype(jnp.bfloat16)
-
-    def result_copy(target, slot):
-        return pltpu.make_async_remote_copy(
-            src_ref=sent16.at[target],
-            dst_ref=got16.at[slot],
-            send_sem=res_send.at[target],
-            recv_sem=res_recv.at[slot],
-            device_id=place(target),
-            device_id_type=MESH,
-        )
-
-    def send_result(d, carry):
-        result_copy((me + d) % total, me).start()
-        return carry
-
-    lax.fori_loop(1, total, send_result, 0)
-    got16[me] = sent16[me]
-
-    labels = lax.broadcasted_iota(jnp.int32, (experts, ids_ref.shape[1]), 0)
-    chosen = jnp.where(ids_ref[...] == labels, weight_ref[...].astype(jnp.float32), 0.0)
-    mix = jnp.broadcast_to(jnp.sum(chosen, axis=1, keepdims=True), (experts, LANES))
-
-    def wait_result(d, carry):
-        other = (me + d) % total
-        result_copy(other, other).wait_recv()
-        return carry
-
-    lax.fori_loop(1, total, wait_result, 0)
-
-    mixed = jnp.zeros((pitch, LANES), jnp.float32)
-    for e in range(experts):
-        both = got16[e * groups].astype(jnp.float32)
-        for g in range(1, groups):
-            both += got16[e * groups + g].astype(jnp.float32)
-        mixed += mix[e : e + 1, :] * both
-    for j in range(blocks):
-        out_ref[:, j * LANES : (j + 1) * LANES] = mixed[j : j + 1, :].astype(jnp.bfloat16)
-
-    def wait_sends(d, carry):
-        other = (me + d) % total
-        token_copy(other, me).wait_send()
-        result_copy(other, me).wait_send()
-        return carry
-
-    lax.fori_loop(1, total, wait_sends, 0)
+        ready = (p + 1) * (step // LANES)
+        while flushed < bands and ready >= min((flushed + 1) * BAND, blocks):
+            low = flushed * BAND
+            for t in range(total):
+                sent16[t // (groups * cores), t // groups % cores, t % groups, low : low + BAND] = (
+                    rows32[t * pitch + low : t * pitch + low + BAND, :].astype(jnp.bfloat16)
+                )
+            pair_copy(flushed).start()
+            flushed += 1
+    for b in range(bands):
+        pass_on(b)
+
+    for b in range(bands):
+
+        def wait_result(d, carry):
+            slot = other_chip(d)
+            result_copy(slot, b, chip_of(slot)).wait_recv()
+            return carry
+
+        lax.fori_loop(1, chips, wait_result, 0)
+        rows = slice(b * BAND, (b + 1) * BAND)
+        mixed = got16[0, rows].astype(jnp.float32)
+        for h in range(1, chips):
+            mixed += got16[h, rows].astype(jnp.float32)
+        for j in range(b * BAND, min((b + 1) * BAND, blocks)):
+            out_ref[:, j * LANES : (j + 1) * LANES] = mixed[
+                j - b * BAND : j - b * BAND + 1, :
+            ].astype(jnp.bfloat16)
+
+    for copy in sends:
+        copy.wait_send()
+    for b in range(bands):
+        pair_copy(b).wait_send()
+
+        def wait_sends(d, carry):
+            result_copy(other_chip(d), b, my_chip).wait_send()
+            return carry
+
+        lax.fori_loop(1, chips, wait_sends, 0)
 
 
 def small_body(tokens, gate_weights, expert_ids, gate_proj, up_proj, down_proj):
@@ -267,7 +368,7 @@
     top_count = expert_ids.shape[3]
     hidden_count = gate_proj.shape[2]
     blocks = features // LANES
-    pitch = -(-blocks // 16) * 16
+    pitch = -(-(blocks + 1) // BAND) * BAND
     pieces = max(p for p in (7, 4, 2, 1) if blocks % p == 0)
     vmem = pl.BlockSpec(memory_space=pltpu.VMEM)
     hbm = pl.BlockSpec(memory_space=pl.ANY)
@@ -286,15 +387,21 @@
             pltpu.VMEM((total, pitch, LANES), jnp.bfloat16),
             pltpu.VMEM((total * pitch, LANES), jnp.float32),
             pltpu.VMEM((total, features), jnp.bfloat16),
-            pltpu.VMEM((total, pitch, LANES), jnp.bfloat16),
-            pltpu.VMEM((total, pitch, LANES), jnp.bfloat16),
+            pltpu.VMEM((experts // 2, 2, groups, pitch, LANES), jnp.bfloat16),
+            pltpu.VMEM((experts // 2, groups, pitch, LANES), jnp.bfloat16),
+            pltpu.VMEM((total // 2, pitch, LANES), jnp.bfloat16),
+            pltpu.VMEM((total // 2, pitch, LANES), jnp.bfloat16),
             dma((pieces,)),
             dma((pieces,)),
             dma((pieces,)),
+            dma((experts // 4,)),
+            dma((experts // 4 * (2 * groups - 1),)),
             dma((total,)),
             dma((total,)),
-            dma((total,)),
-            dma((total,)),
+            dma((pitch // BAND,)),
+            dma((pitch // BAND,)),
+            dma((total // 2, pitch // BAND)),
+            dma((total // 2, pitch // BAND)),
         ],
         compiler_params=pltpu.CompilerParams(collective_id=0, has_side_effects=True),
     )(
@@ -313,7 +420,7 @@
     total = groups * lax.axis_size("ep")
     held = 3 * gate_proj.size * gate_proj.dtype.itemsize
     one_each = tokens.shape[2] == 1 and tokens.shape[3] % LANES == 0
-    fits = total <= 64 and total % 16 == 0 and held <= 36 << 20
+    fits = total <= 64 and total % 16 == 0 and lax.axis_size("ep") % 4 == 0 and held <= 36 << 20
     few = groups <= groups * expert_ids.shape[3] // lax.axis_size("ep") + 1
     form = small_body if one_each and fits and few else body
     return form(tokens, gate_weights, expert_ids, gate_proj, up_proj, down_proj)

time: 30.8 us -> 29.8 us (0.968)
  Pallas kernels: 29 us -> 28.3 us
    pallas_call x1, Pallas kernels: 29 us -> 28.3 us  [small_body(): pl.pallas_call(functools.partial(kernel, groups, experts, pieces), out_sh...]
where the time goes in v2:
time: 29.8 us; the launch traced here: 29.6 us
  Pallas kernels  28.3 us (95%)
  local copies, waits for them, and re-layouts  1.33 us (4%)
    pallas_call x1, Pallas kernels, small_body(): pl.pallas_call(functools.partial(kernel, groups, experts, pieces), out_sh...  28.3 us
    unnamed x1, local copies, waits for them, and re-layouts  1.33 us

profile of v2, /device:TPU:0, one launch (start us, length us, event | category | flops | bytes accessed | tf_op | source)
XLA Modules:
  0.0 29.6 jit_solution(11741264076401956668)
XLA Ops:
  0.0 28.3 %shard_map.64 = bf16[1,3584]{1,0:T(2,128)(2,1)} custom-call(bf16[1,3584]{1,0:T(2,128)(2,1)} %bitcast.11, bf16[1,8]{1,0:T(2,128)(2,1)} %bitcast.12, s32[1,8]{1,0:T(1,128)} %bitcast.13, bf16[3584,1024]{1,0:T(8,128)(2,1)} %bitcast.7, bf16[3584,1024]{1,0:T(8,128)(2,1)} %bitcast.8, bf16[1024,3584]{1,0:T(8,128)(2,1)} %bitcast.9), custom_call_target="tpu_custom_call" | custom-call | tf_op jit(solution)/shard_map/pallas_call | solution.py:376
  28.3 1.3 %copy.8 = bf16[1,1,1,3584]{3,2,1,0:T(2,128)(2,1)} copy(bf16[1,1,1,3584]{3,2,1,0:T(2,128)(2,1)} %bitcast.10) | data formatting | bytes 14336
